TPU v7x, 32 devices: a whole 2x2x4 slice. The times are simulated.
32 devices in a mesh: dp: 8 (over z, x), mp: 4 (over y, core).
Axes of the slice: x: 2, y: 2, z: 4, core: 2. Of those that a mesh axis runs over, the one named last changes fastest.
Arguments:
- query_rows: bfloat16 [512, 2560], P('dp', 'mp'), may hold values from -48 to 48
- doc_rows: bfloat16 [512, 2560], P('dp', 'mp'), may hold values from -48 to 48
- head: bfloat16 [2560, 2560], P(None, 'mp'), may hold values from -0.125 to 0.125
- logit_scale: float32 [7], replicated, may hold values from 1 to 3
- loss_grad: float32 [512, 7], P('dp'), may hold values from 0.5 to 2
- shortlist: int32 [512, 128], P('dp'), may hold values from 0 to 127, as said below
- send_rows: int32 [8, 128], P('dp'), may hold values from -1 to 63, as said below
Outputs:
- query_grad: bfloat16 [512, 2560], P('dp', 'mp')
- doc_grad: bfloat16 [512, 2560], P('dp', 'mp')
- head_grad: float32 [2560, 2560], P('dp', 'mp')
Inputs may be any that keep to these rules, and one draw needn't show every extreme that they name: shortlist[i, n] is a slot o * 16 + j of the rows fetched for the owner of query i, and send_rows at place j of the block owner o sends to that owner is never -1. send_rows[o, r * 16 + j] is a row among owner o's 64 documents, sent to owner r at place j; in each block of 16 places the rows are distinct and come first, -1 fills the rest; the block an owner sends to itself is always full.
All inputs are finite; a program needn't handle non-finite values.
Results may differ from a plain program's by a relative error of at most 0.014.
The roundings to bfloat16 on the way count: a program that leaves them out, or rounds other values in their place, can miss the bound.
Values may be sent and summed in bfloat16 or wider, within the bound.
A program may use at most 64 MiB of HBM per device.

v0:
```python
import functools
import math

import jax
import jax.numpy as jnp
from jax import lax
from jax.experimental import pallas as pl
from jax.experimental.pallas import tpu as pltpu
from jax.sharding import PartitionSpec as P

NW = 7
MESH = pl.DeviceIdType.MESH
BF = jnp.bfloat16
F32 = jnp.float32


def width_bounds(feature_total):
    return [0] + [feature_total // 2 ** (NW - 1 - level) for level in range(NW)]


def flip_bits(value, mask):
    bit = 1
    while bit <= mask:
        if mask & bit:
            value = value + bit - 2 * bit * lax.rem(lax.div(value, bit), 2)
        bit *= 2
    return value


def kernel(
    n_dp,
    n_mp,
    q_hbm,
    d_hbm,
    head_hbm,
    scale_hbm,
    weight_hbm,
    short_hbm,
    rows_hbm,
    qg_ref,
    dg_ref,
    hg_ref,
    q_ref,
    d_ref,
    scale_ref,
    weight_ref,
    short_ref,
    rows_ref,
    head,
    whole,
    own_t,
    rows_t,
    f_out,
    f_in,
    ex_out,
    ex_in,
    r_out,
    r_in,
    grads,
    part_out,
    part_in,
    flat,
    ssem,
    rsem,
    lsem,
):
    ql, cols = q_ref.shape
    total = n_mp * cols
    slots = rows_ref.shape[1]
    blk = slots // n_dp
    chunk = total // n_dp
    per_mp = n_dp // n_mp
    half = n_dp // 2
    bounds = width_bounds(total)
    r = lax.axis_index("dp")
    m = lax.axis_index("mp")
    partner = flip_bits(r, 1)

    counts = {}

    def alloc(kind, n):
        start = counts.get(kind, 0)
        counts[kind] = start + n
        return start

    def remote(src, dst, s, t, **where):
        return pltpu.make_async_remote_copy(
            src_ref=src,
            dst_ref=dst,
            send_sem=ssem.at[s],
            recv_sem=rsem.at[t],
            device_id=where,
            device_id_type=MESH,
        )

    loads = [
        pltpu.make_async_copy(src, dst, lsem.at[2 + i])
        for i, (src, dst) in enumerate(
            [
                (d_hbm, d_ref),
                (q_hbm, q_ref),
                (rows_hbm, rows_ref),
                (short_hbm, short_ref),
                (weight_hbm, weight_ref),
                (scale_hbm, scale_ref),
            ]
        )
    ]
    for copy in loads:
        copy.start()
    head_copy = pltpu.make_async_copy(head_hbm, head, lsem.at[0])
    head_copy.start()
    barrier = pltpu.get_barrier_semaphore()
    for j in range(1, n_mp):
        pl.semaphore_signal(
            barrier, inc=1, device_id={"mp": flip_bits(m, j)}, device_id_type=MESH
        )
    for k in range(1, n_dp):
        pl.semaphore_signal(
            barrier, inc=1, device_id={"dp": lax.rem(r + k, n_dp)}, device_id_type=MESH
        )
    for copy in loads:
        copy.wait()
    pl.semaphore_wait(barrier, n_mp - 1 + n_dp - 1)

    sent = []

    s0 = alloc("s", 2 * (n_mp - 1))
    t0 = alloc("r", 2 * (n_mp - 1))
    row_copies = []
    for h, ref in enumerate((d_ref, q_ref)):
        base = h * (n_mp - 1) - 1
        copies = {}
        for j in [*range(2, n_mp, 2), 1]:
            copies[j] = remote(
                ref, whole.at[m, h], s0 + base + j, t0 + base + j, mp=flip_bits(m, j)
            )
            copies[j].start()
        for j in range(2, n_mp, 2):
            k = flip_bits(m, j)
            copies[j + 1] = remote(
                whole.at[k, h],
                whole.at[k, h],
                s0 + base + j + 1,
                t0 + base + j + 1,
                mp=flip_bits(m, 1),
            )
        row_copies.append(copies)
        sent.extend(copies.values())

    own = jnp.concatenate([d_ref[...], q_ref[...]], axis=0)
    own_t[...] = jnp.transpose(own)
    s_t = alloc("s", per_mp)
    t_t = alloc("r", n_dp)

    def spread(c):
        target = m * per_mp + c
        lane = pl.ds(pl.multiple_of(r * 2 * ql, 2 * ql), 2 * ql)
        src = own_t.at[pl.ds(c * chunk, chunk)]
        dst = rows_t.at[:, lane]
        return (
            target,
            remote(src, dst, s_t + c, t_t + r, dp=target),
            pltpu.make_async_copy(src, dst, lsem.at[1]),
        )

    for c in range(per_mp):
        target, copy, local = spread(c)

        @pl.when(target != r)
        def _(copy=copy):
            copy.start()

        @pl.when(target == r)
        def _(local=local):
            local.start()

    head_copy.wait()

    def head_rows(k):
        return head[pl.ds(pl.multiple_of(k * cols, cols), cols), :]

    def project(h, ref):
        copies = row_copies[h]
        acc = jnp.dot(ref[...], head_rows(m), preferred_element_type=F32)
        for j in range(1, n_mp, 2):
            for i in [j] if j == 1 else [j - 1, j]:
                k = flip_bits(m, i)
                copies[i].wait_recv()
                if i % 2 == 0:
                    copies[i + 1].start()
                acc = acc + jnp.dot(whole[k, h], head_rows(k), preferred_element_type=F32)
        return acc.astype(BF)

    slot_ids = lax.broadcasted_iota(jnp.int32, (ql, slots), 1)
    row_ids = lax.broadcasted_iota(jnp.int32, (ql, slots), 0)
    eye = slot_ids == row_ids
    sel_t32 = jnp.where(rows_ref[...] == row_ids, 1.0, 0.0)
    sel_t = sel_t32.astype(BF)
    sel = jnp.transpose(sel_t32).astype(BF)
    doc = project(0, d_ref)

    def to_blocks(values, out):
        if blk % 16 == 0:
            out[...] = values.astype(BF).reshape(n_dp, blk, cols)
        else:
            flat[...] = values
            for p in range(n_dp):
                out[p] = flat[p * blk : (p + 1) * blk, :].astype(BF)

    def from_blocks(buf):
        if blk % 16 == 0:
            return buf[...].reshape(slots, cols)
        for p in range(n_dp):
            flat[p * blk : (p + 1) * blk, :] = buf[p].astype(F32)
        return flat[...].astype(BF)

    def exchange(out, into):
        s = alloc("s", n_dp - 1)
        t = alloc("r", n_dp - 1)
        copies = []
        for k in range(1, n_dp):
            peer = lax.rem(r + k, n_dp)
            copy = remote(out.at[peer], into.at[r], s + k - 1, t + k - 1, dp=peer)
            copy.start()
            copies.append(copy)
            sent.append(copy)
        into[r] = out[r]
        return copies

    to_blocks(jnp.dot(sel, doc, preferred_element_type=F32), f_out)
    fetches = exchange(f_out, f_in)
    query = project(1, q_ref)

    short = short_ref[...]
    named = jnp.zeros((ql, slots), F32)
    for n in range(short.shape[1]):
        named = named + jnp.where(short[:, n : n + 1] == slot_ids, 1.0, 0.0)

    col_ids = m * cols + lax.broadcasted_iota(jnp.int32, (1, cols), 1)
    below = [jnp.where(col_ids < b, 1.0, 0.0) for b in bounds]
    seg = [below[s + 1] - below[s] for s in range(NW)]
    q_prefix = jnp.concatenate([query * below[w + 1].astype(BF) for w in range(NW - 1)], axis=0)
    zero_q = jnp.zeros_like(query)
    q_seg = jnp.concatenate([query * seg[s].astype(BF) for s in range(NW)] + [zero_q], axis=0)

    for copy in fetches:
        copy.wait_recv()
    fetched = from_blocks(f_in)
    against = jnp.concatenate([fetched] + [doc] * (slots // ql), axis=0)
    rhs_t = (((1,), (1,)), ((), ()))
    top = lax.dot_general(query, against, rhs_t, preferred_element_type=F32)
    pos_row = jnp.sum(jnp.where(eye, top[:, slots:], 0.0), axis=0, keepdims=True)
    ex_out[0:ql, :] = top[:, :slots]
    ex_out[ql:, :] = jnp.broadcast_to(pos_row, (8, slots))
    s1 = alloc("s", n_mp - 1)
    t1 = alloc("r", n_mp - 1)
    shares = []
    for j in range(1, n_mp):
        copy = remote(ex_out, ex_in.at[m], s1 + j - 1, t1 + j - 1, mp=flip_bits(m, j))
        copy.start()
        shares.append(copy)
        sent.append(copy)

    s_f = alloc("s", n_mp - 1)
    t_f = alloc("r", 1)
    keeper = lax.div(r, per_mp)
    same = lax.rem(m, 2) == lax.rem(keeper, 2)
    passes = jnp.logical_and(same, m != keeper)
    forwards = [
        remote(rows_t, rows_t, s_f + j - 1, t_f, mp=flip_bits(m, j))
        for j in [*range(2, n_mp, 2), 1]
    ]

    @pl.when(m == keeper)
    def _():
        pltpu.make_async_copy(
            own_t.at[pl.ds(0, chunk)], rows_t.at[:, pl.ds(0, 2 * ql)], lsem.at[1]
        ).wait()
        for p in range(n_dp):

            @pl.when(r != p)
            def _(p=p):
                remote(
                    own_t.at[pl.ds(0, chunk)],
                    rows_t.at[:, pl.ds(p * 2 * ql, 2 * ql)],
                    s_t,
                    t_t + p,
                    dp=r,
                ).wait_recv()

        for copy in forwards:
            copy.start()

    scores = lax.dot_general(q_prefix, against, rhs_t, preferred_element_type=F32)
    levels = [scores[w * ql : (w + 1) * ql] for w in range(NW - 1)] + [top]
    neg = [level[:, :slots] for level in levels]
    pos = [
        jnp.sum(jnp.where(eye, level[:, slots:], 0.0), axis=1, keepdims=True)
        for level in levels
    ]
    for j in range(1, n_mp):
        k = flip_bits(m, j)
        shares[j - 1].wait_recv()
        share = ex_in[k]
        other_neg = share[0:ql]
        other_pos = jnp.sum(
            jnp.where(eye, jnp.broadcast_to(share[ql : ql + 1], (ql, slots)), 0.0),
            axis=1,
            keepdims=True,
        )
        for w in range(NW):
            inside = jnp.where((k + 1) * cols <= bounds[w + 1], 1.0, 0.0)
            neg[w] = neg[w] + inside * other_neg
            pos[w] = pos[w] + inside * other_pos

    weight = jnp.transpose(weight_ref[...])
    seg_neg = [None] * NW
    seg_pos = [None] * NW
    run_neg = jnp.zeros((ql, slots), F32)
    run_pos = jnp.zeros((ql, 1), F32)
    for w in reversed(range(NW)):
        scale = scale_ref[w] * (1.0 / math.sqrt(bounds[w + 1]))
        neg_logit = jnp.where(named > 0.0, neg[w] * scale, -1e30)
        pos_logit = pos[w] * scale
        highest = jnp.maximum(jnp.max(neg_logit, axis=1, keepdims=True), pos_logit)
        neg_exp = named * jnp.exp(neg_logit - highest)
        pos_exp = jnp.exp(pos_logit - highest)
        denominator = jnp.sum(neg_exp, axis=1, keepdims=True) + pos_exp
        row_weight = weight[:, w : w + 1] * scale
        run_neg = run_neg + neg_exp * (row_weight / denominator)
        run_pos = run_pos + row_weight * (pos_exp / denominator - 1.0)
        seg_neg[w] = run_neg
        seg_pos[w] = run_pos

    coeff = jnp.concatenate(seg_neg + [jnp.zeros((ql, slots), F32)], axis=0)
    coeff_t = jnp.transpose(coeff).astype(BF)
    back = jnp.dot(coeff_t, q_seg, preferred_element_type=F32)
    to_blocks(back, r_out)
    returns = exchange(r_out, r_in)

    levels = jnp.dot(coeff[: NW * ql].astype(BF), fetched, preferred_element_type=F32)
    pos_cols = jnp.zeros((ql, cols), F32)
    grad = jnp.zeros((ql, cols), F32)
    for s in range(NW):
        grad = grad + levels[s * ql : (s + 1) * ql] * seg[s]
        pos_cols = pos_cols + seg_pos[s] * seg[s]
    grad_q = (grad + pos_cols * doc.astype(F32)).astype(BF)

    def gather_start(h, value):
        grads[r, h] = value
        s = alloc("s", n_dp - 1)
        t = alloc("r", n_dp - 1)
        direct = []
        for k in range(1, half):
            peer = flip_bits(r, 2 * k)
            direct.append(
                remote(grads.at[r, h], grads.at[r, h], s + k - 1, t + k - 1, dp=peer)
            )
        side = [
            remote(grads.at[r, h], grads.at[r, h], s + half - 1, t + half - 1, dp=partner)
        ]
        for k in range(1, half):
            src = flip_bits(r, 2 * k)
            side.append(
                remote(
                    grads.at[src, h],
                    grads.at[src, h],
                    s + half - 1 + k,
                    t + half - 1 + k,
                    dp=partner,
                )
            )
        for copy in direct:
            copy.start()
        side[0].start()
        sent.extend(direct + side)
        return direct, side

    def gather_forward(gather, steps):
        direct, side = gather
        for k in steps:
            direct[k - 1].wait_recv()
            side[k].start()

    def partial_start(h, value, after_first=None, before_mine=None):
        s = alloc("s", n_mp - 1)
        t = alloc("r", n_mp - 1)
        copies = []
        for j in range(1, n_mp):
            k = flip_bits(m, j)
            term = lax.dot_general(
                value, head_rows(k), (((1,), (1,)), ((), ())), preferred_element_type=F32
            )
            part_out[h, j - 1] = term.astype(BF)
            copy = remote(
                part_out.at[h, j - 1], part_in.at[h, j - 1], s + j - 1, t + j - 1, mp=k
            )
            copy.start()
            copies.append(copy)
            sent.append(copy)
            if j == 1 and after_first is not None:
                after_first()
        if before_mine is not None:
            before_mine()
        mine = lax.dot_general(
            value, head_rows(m), (((1,), (1,)), ((), ())), preferred_element_type=F32
        )
        return copies, mine

    def partial_end(h, copies, mine):
        for j in range(1, n_mp):
            copies[j - 1].wait_recv()
            mine = mine + part_in[h, j - 1].astype(F32)
        return mine.astype(BF)

    gather_q = gather_start(1, grad_q)
    part_q = partial_start(1, grad_q)

    for copy in returns:
        copy.wait_recv()
    doc_back = jnp.dot(sel_t, from_blocks(r_in), preferred_element_type=F32)
    grad_d = (doc_back + pos_cols * query.astype(F32)).astype(BF)
    gather_d = gather_start(0, grad_d)

    def between():
        @pl.when(passes)
        def _():
            forwards[-1].wait_recv()
            forwards[-1].start()

        gather_forward(gather_d, range(1, min(2, half)))

    part_d = partial_start(
        0, grad_d, lambda: gather_forward(gather_q, range(1, half)), between
    )
    gather_forward(gather_d, range(2, half))

    @pl.when(jnp.logical_not(same))
    def _():
        forwards[-1].wait_recv()

    qg_ref[...] = partial_end(1, *part_q)

    depth = 4 * ql
    for k in range(half):
        pair = lax.div(flip_bits(r, 2 * k), 2)
        gather_q[1][k].wait_recv()
        gather_d[1][k].wait_recv()
        lanes = pl.ds(pl.multiple_of(pair * depth, depth), depth)
        term = jnp.dot(
            rows_t[:, lanes],
            grads[pl.ds(pair * 2, 2)].reshape(depth, cols),
            preferred_element_type=F32,
        )
        if k == 0:
            hg_ref[...] = term
        else:
            hg_ref[...] += term
        if k == max(half - 2, 0):
            dg_ref[...] = partial_end(0, *part_d)

    for copy in sent:
        copy.wait_send()
    for c in range(per_mp):
        target, copy, _ = spread(c)

        @pl.when(target != r)
        def _(copy=copy):
            copy.wait_send()

    @pl.when(m == keeper)
    def _():
        for copy in forwards:
            copy.wait_send()

    @pl.when(passes)
    def _():
        forwards[-1].wait_send()


def hand_on(*refs):
    for src, dst in zip(refs[: len(refs) // 2], refs[len(refs) // 2 :]):
        dst[...] = src[...]


def solution(mesh):
    n_dp = mesh.shape["dp"]
    n_mp = mesh.shape["mp"]

    def on_device(query_rows, doc_rows, head, logit_scale, loss_grad, shortlist, send_rows):
        ql, cols = query_rows.shape
        total = n_mp * cols
        slots = send_rows.shape[1]
        blk = slots // n_dp
        chunk = total // n_dp
        n_send = 2 * (n_mp - 1) + n_dp // n_mp + 4 * (n_dp - 1) + 4 * (n_mp - 1)
        n_recv = 2 * (n_mp - 1) + n_dp + 4 * (n_dp - 1) + 3 * (n_mp - 1) + 1
        vmem = pl.BlockSpec(memory_space=pltpu.VMEM)
        shapes = (
            jax.ShapeDtypeStruct((ql, cols), BF),
            jax.ShapeDtypeStruct((ql, cols), BF),
            jax.ShapeDtypeStruct((chunk, cols), F32),
        )
        found = pl.pallas_call(
            functools.partial(kernel, n_dp, n_mp),
            out_shape=shapes,
            in_specs=[pl.BlockSpec(memory_space=pltpu.HBM)] * 7,
            out_specs=(vmem, vmem, vmem),
            scratch_shapes=[
                pltpu.VMEM((ql, cols), BF),
                pltpu.VMEM((ql, cols), BF),
                pltpu.SMEM(logit_scale.shape, F32),
                pltpu.VMEM(loss_grad.shape[::-1], F32),
                pltpu.VMEM(shortlist.shape, jnp.int32),
                pltpu.VMEM(send_rows.shape, jnp.int32),
                pltpu.VMEM((total, cols), BF),
                pltpu.VMEM((n_mp, 2, ql, cols), BF),
                pltpu.VMEM((cols, 2 * ql), BF),
                pltpu.VMEM((chunk, n_dp * 2 * ql), BF),
                pltpu.VMEM((n_dp, blk, cols), BF),
                pltpu.VMEM((n_dp, blk, cols), BF),
                pltpu.VMEM((ql + 8, slots), F32),
                pltpu.VMEM((n_mp, ql + 8, slots), F32),
                pltpu.VMEM((n_dp, blk, cols), BF),
                pltpu.VMEM((n_dp, blk, cols), BF),
                pltpu.VMEM((n_dp, 2, ql, cols), BF),
                pltpu.VMEM((2, n_mp - 1, ql, cols), BF),
                pltpu.VMEM((2, n_mp - 1, ql, cols), BF),
                pltpu.VMEM((slots, cols), F32),
                pltpu.SemaphoreType.DMA((n_send,)),
                pltpu.SemaphoreType.DMA((n_recv,)),
                pltpu.SemaphoreType.DMA((8,)),
            ],
            compiler_params=pltpu.CompilerParams(
                collective_id=0, has_side_effects=True, vmem_limit_bytes=32 << 20
            ),
        )(
            *[
                pltpu.with_memory_space_constraint(x, pltpu.HBM)
                for x in (
                    query_rows,
                    doc_rows,
                    head,
                    logit_scale,
                    loss_grad.T,
                    shortlist,
                    send_rows,
                )
            ]
        )
        return pl.pallas_call(
            hand_on,
            out_shape=shapes,
            in_specs=[vmem] * 3,
            out_specs=(vmem,) * 3,
            compiler_params=pltpu.CompilerParams(vmem_limit_bytes=8 << 20),
        )(*found)

    return jax.shard_map(
        on_device,
        mesh=mesh,
        in_specs=(
            P("dp", "mp"),
            P("dp", "mp"),
            P(None, "mp"),
            P(),
            P("dp", None),
            P("dp", None),
            P("dp", None),
        ),
        out_specs=(P("dp", "mp"), P("dp", "mp"), P("dp", "mp")),
        check_vma=False,
    )
```

profile of v0, /device:TPU:0, one launch (start us, length us, event | category | flops | bytes accessed | tf_op | source)
XLA Modules:
  0.0 48.6 jit_solution(5575169791998811437)
XLA Ops:
  0.6 46.9 %shard_map.94 = (bf16[64,640]{1,0:T(8,128)(2,1)S(1)}, bf16[64,640]{1,0:T(8,128)(2,1)S(1)}, f32[320,640]{1,0:T(8,128)S(1)}) custom-call(bf16[64,640]{1,0:T(8,128)(2,1)} %q_hbm.1, bf16[64,640]{1,0:T(8,128)(2,1)} %d_hbm.1, bf16[2560,640]{1,0:T(8,128)(2,1)} %head_hbm.1, f32[7]{0:T(128)} %scale_hbm.1, f32[7,64]{1,0:T(8,128)} %bitcast.1, s32[64,128]{1,0:T(8,128)} %short_hbm.1, ...), custom_call_target="tpu_custom_call" | custom-call | tf_op jit(solution)/shard_map/pallas_call | solution.py:505
  47.6 1.0 %shard_map.95 = (bf16[64,640]{1,0:T(8,128)(2,1)}, bf16[64,640]{1,0:T(8,128)(2,1)}, f32[320,640]{1,0:T(8,128)}) custom-call(bf16[64,640]{1,0:T(8,128)(2,1)S(1)} %get-tuple-element.6.refs_0_, bf16[64,640]{1,0:T(8,128)(2,1)S(1)} %get-tuple-element.7.refs_1_, f32[320,640]{1,0:T(8,128)S(1)} %get-tuple-element.8.refs_2_), custom_call_target="tpu_custom_call" | custom-call | tf_op jit(solution)/shard_map/pallas_call | solution.py:552
where the time goes:
time: 48.7 us; the launch traced here: 48.6 us
  Pallas kernels  48 us (99%)
  between operations  0.64 us (1%)
    pallas_call x1, Pallas kernels, on_device(): pl.pallas_call(functools.partial(kernel, n_dp, n_mp), out_shape=shapes, i...  46.9 us
    pallas_call x1, Pallas kernels, on_device(): pl.pallas_call(hand_on, out_shape=shapes, in_specs=[vmem] * 3, out_specs=...  1.01 us

commit v1 on v0

v1 whole, which is shorter than its diff:
```python
import functools
import math

import jax
import jax.numpy as jnp
from jax import lax
from jax.experimental import pallas as pl
from jax.experimental.pallas import tpu as pltpu
from jax.sharding import PartitionSpec as P

NW = 7
PARTS = 2
MESH = pl.DeviceIdType.MESH
BF = jnp.bfloat16
F32 = jnp.float32


def width_bounds(feature_total):
    return [0] + [feature_total // 2 ** (NW - 1 - level) for level in range(NW)]


def local_segments(bounds, cols):
    return sum(bound <= cols for bound in bounds[1:])


def flip_bits(value, mask):
    bit = 1
    while bit <= mask:
        if mask & bit:
            value = value + bit - 2 * bit * lax.rem(lax.div(value, bit), 2)
        bit *= 2
    return value


def kernel(
    n_dp,
    n_mp,
    q_hbm,
    d_hbm,
    head_hbm,
    scale_hbm,
    weight_hbm,
    short_hbm,
    rows_hbm,
    qg_ref,
    dg_ref,
    hg_ref,
    q_ref,
    d_ref,
    scale_ref,
    weight_ref,
    short_ref,
    rows_ref,
    head,
    whole,
    own_t,
    rows_t,
    f_out,
    f_in,
    ex_out,
    ex_in,
    coef,
    r_out,
    r_in,
    grads,
    part_out,
    part_in,
    flat,
    ssem,
    rsem,
    lsem,
):
    ql, cols = q_ref.shape
    total = n_mp * cols
    slots = rows_ref.shape[1]
    blk = slots // n_dp
    chunk = total // n_dp
    per_mp = n_dp // n_mp
    half = n_dp // 2
    bounds = width_bounds(total)
    n_loc = local_segments(bounds, cols)
    r = lax.axis_index("dp")
    m = lax.axis_index("mp")
    partner = flip_bits(r, 1)

    counts = {}

    def alloc(kind, n):
        start = counts.get(kind, 0)
        counts[kind] = start + n
        return start

    def remote(src, dst, s, t, **where):
        return pltpu.make_async_remote_copy(
            src_ref=src,
            dst_ref=dst,
            send_sem=ssem.at[s],
            recv_sem=rsem.at[t],
            device_id=where,
            device_id_type=MESH,
        )

    loads = [
        pltpu.make_async_copy(src, dst, lsem.at[2 + i])
        for i, (src, dst) in enumerate(
            [
                (d_hbm, d_ref),
                (q_hbm, q_ref),
                (rows_hbm, rows_ref),
                (short_hbm, short_ref),
                (weight_hbm, weight_ref),
                (scale_hbm, scale_ref),
            ]
        )
    ]
    for copy in loads:
        copy.start()
    head_copy = pltpu.make_async_copy(head_hbm, head, lsem.at[0])
    head_copy.start()
    barrier = pltpu.get_barrier_semaphore()
    for j in range(1, n_mp):
        pl.semaphore_signal(
            barrier, inc=1, device_id={"mp": flip_bits(m, j)}, device_id_type=MESH
        )
    for k in range(1, n_dp):
        pl.semaphore_signal(
            barrier, inc=1, device_id={"dp": lax.rem(r + k, n_dp)}, device_id_type=MESH
        )
    for copy in loads:
        copy.wait()
    pl.semaphore_wait(barrier, n_mp - 1 + n_dp - 1)

    sent = []
    parts = PARTS

    s0 = alloc("s", 2 * (n_mp - 1))
    t0 = alloc("r", 2 * (n_mp - 1))
    row_copies = []
    for h, ref in enumerate((d_ref, q_ref)):
        base = h * (n_mp - 1) - 1
        copies = {}
        for j in [*range(2, n_mp, 2), 1]:
            copies[j] = remote(
                ref, whole.at[m, h], s0 + base + j, t0 + base + j, mp=flip_bits(m, j)
            )
            copies[j].start()
        for j in range(2, n_mp, 2):
            k = flip_bits(m, j)
            copies[j + 1] = remote(
                whole.at[k, h],
                whole.at[k, h],
                s0 + base + j + 1,
                t0 + base + j + 1,
                mp=flip_bits(m, 1),
            )
        row_copies.append(copies)
        sent.extend(copies.values())

    def exchange(out, into):
        s = alloc("s", n_dp - 1)
        t = alloc("r", n_dp - 1)
        copies = []
        for k in range(1, n_dp):
            peer = lax.rem(r + k, n_dp)
            copy = remote(out(peer), into(peer), s + k - 1, t + k - 1, dp=peer)
            copy.start()
            copies.append(copy)
            sent.append(copy)
        return copies

    own = jnp.concatenate([d_ref[...], q_ref[...]], axis=0)
    own_t[...] = jnp.transpose(own)
    s_t = alloc("s", per_mp)
    t_t = alloc("r", n_dp)
    place = lax.div(r, 2)
    side = lax.rem(r, 2)
    keeper = lax.div(r, per_mp)

    def spread(late, step):
        for i in range(per_mp // 2):
            c = 2 * i + (1 - side if late else side)
            target = m * per_mp + c
            copy = remote(
                own_t.at[pl.ds(pl.multiple_of(c * chunk, 16), chunk)],
                rows_t.at[side, place],
                s_t + 2 * i + int(late),
                t_t + r,
                dp=target,
            )
            if late:
                step(copy)
            else:
                pl.when(target != r)(functools.partial(step, copy))

    spread(False, lambda copy: copy.start())

    @pl.when(m == keeper)
    def _():
        c = lax.rem(r, per_mp)
        rows_t[side, place] = own_t[pl.ds(pl.multiple_of(c * chunk, 16), chunk), :]

    s_f = alloc("s", 2 * (n_mp - 1))
    t_f = alloc("r", 2)
    same = lax.rem(m, 2) == lax.rem(keeper, 2)
    passes = jnp.logical_and(same, m != keeper)

    def hand_over(late):
        ref = rows_t.at[1 - side if late else side]
        first = s_f + int(late) * (n_mp - 1) - 1
        return [
            remote(ref, ref, first + j, t_f + int(late), mp=flip_bits(m, j))
            for j in [*range(2, n_mp, 2), 1]
        ]

    halves = [hand_over(False), hand_over(True)]

    def hand_start(late):
        @pl.when(m == keeper)
        def _():
            for p in range(half):
                origin = 2 * p + (1 - side if late else side)

                @pl.when(r != origin)
                def _(p=p, origin=origin):
                    remote(
                        own_t.at[pl.ds(0, chunk)],
                        rows_t.at[1 - side if late else side, p],
                        s_t,
                        t_t + origin,
                        dp=r,
                    ).wait_recv()

            for copy in halves[late]:
                copy.start()

    def hand_pass(late):
        @pl.when(passes)
        def _():
            halves[late][-1].wait_recv()
            halves[late][-1].start()

    def hand_end(late):
        @pl.when(jnp.logical_not(same))
        def _():
            halves[late][-1].wait_recv()

    head_copy.wait()

    def head_rows(k):
        return head[pl.ds(pl.multiple_of(k * cols, cols), cols), :]

    def project(h, ref):
        copies = row_copies[h]
        acc = jnp.dot(ref[...], head_rows(m), preferred_element_type=F32)
        for j in range(1, n_mp, 2):
            for i in [j] if j == 1 else [j - 1, j]:
                k = flip_bits(m, i)
                copies[i].wait_recv()
                if i % 2 == 0:
                    copies[i + 1].start()
                acc = acc + jnp.dot(whole[k, h], head_rows(k), preferred_element_type=F32)
        return acc.astype(BF)

    class Gather:
        def __init__(self, piece, parts):
            self.piece = piece
            self.parts = parts
            self.s = alloc("s", parts * (4 * half - 1))
            self.t = alloc("r", parts * 2 * half)
            self.used = 0
            self.own = [
                ([self.copy(r, c, dz) for c in range(parts)], self.within(dz))
                for dz in (-1, 1)
            ]
            self.across = [self.copy(r, c, 0) for c in range(parts)]
            self.hops = {}
            for d in range(1, half):
                self.hops[d] = []
                for dz in (-1, 1):
                    origin = lax.rem(r - 2 * dz * d + 2 * n_dp, n_dp)
                    steps = [
                        (self.copy(origin, c, dz), self.copy(origin, c, 0))
                        for c in range(parts)
                    ]
                    self.hops[d].append((origin, self.within(-dz * d), self.within(dz), steps))

        def within(self, step):
            return place + step >= 0 if step < 0 else place + step < half

        def copy(self, origin, c, dz):
            ref = self.piece(origin, c)
            row = lax.div(origin, 2) + (half if dz == 0 else 0)
            target = lax.rem(r + 2 * dz + n_dp, n_dp) if dz else partner
            self.used += 1
            return remote(
                ref, ref, self.s + self.used - 1, self.t + row * self.parts + c, dp=target
            )

        def start(self):
            for copies, inside in self.own:

                @pl.when(inside)
                def _(copies=copies):
                    for copy in copies:
                        copy.start()

            for copy in self.across:
                copy.start()

        def forward(self, *hops):
            for d in hops:
                for origin, there, further, steps in self.hops[d]:

                    @pl.when(there)
                    def _(further=further, steps=steps):
                        for relay, over in steps:
                            relay.wait_recv()
                            pl.when(further)(relay.start)
                            over.start()

        def finish(self, line):
            for c in range(self.parts):
                self.copy_from_partner(line, c).wait_recv()

        def copy_from_partner(self, line, c):
            ref = self.piece(line * 2 + 1 - side, c)
            row = self.t + (line + half) * self.parts + c
            return remote(ref, ref, self.s, row, dp=partner)

        def drain(self):
            for copies, inside in self.own:

                @pl.when(inside)
                def _(copies=copies):
                    for copy in copies:
                        copy.wait_send()

            for copy in self.across:
                copy.wait_send()
            for hops in self.hops.values():
                for origin, there, further, steps in hops:

                    @pl.when(there)
                    def _(further=further, steps=steps):
                        for _, over in steps:
                            over.wait_send()

                        @pl.when(further)
                        def _():
                            for relay, _ in steps:
                                relay.wait_send()

    slot_ids = lax.broadcasted_iota(jnp.int32, (ql, slots), 1)
    row_ids = lax.broadcasted_iota(jnp.int32, (ql, slots), 0)
    eye = slot_ids == row_ids
    from_rows = (((0,), (0,)), ((), ()))

    sel_t32 = jnp.where(rows_ref[...] == row_ids, 1.0, 0.0)
    sel_t = sel_t32.astype(BF)
    sel = jnp.transpose(sel_t32).astype(BF)
    doc = project(0, d_ref)

    def to_blocks(values, out):
        if blk % 16 == 0:
            out[...] = values.astype(BF).reshape(n_dp, blk, cols)
        else:
            flat[...] = values
            for p in range(n_dp):
                out[p] = flat[p * blk : (p + 1) * blk, :].astype(BF)

    def from_blocks(buf):
        if blk % 16 == 0:
            return buf[...].reshape(slots, cols)
        for p in range(n_dp):
            flat[p * blk : (p + 1) * blk, :] = buf[p].astype(F32)
        return flat[...].astype(BF)

    to_blocks(jnp.dot(sel, doc, preferred_element_type=F32), f_out)
    fetches = exchange(lambda peer: f_out.at[peer], lambda peer: f_in.at[r])
    f_in[r] = f_out[r]
    query = project(1, q_ref)
    hand_start(0)

    short = short_ref[...]
    named = jnp.zeros((ql, slots), F32)
    for n in range(short.shape[1]):
        named = named + jnp.where(short[:, n : n + 1] == slot_ids, 1.0, 0.0)

    col_ids = lax.broadcasted_iota(jnp.int32, (1, cols), 1)
    seg = [
        jnp.where(jnp.logical_and(col_ids >= bounds[s], col_ids < bounds[s + 1]), 1.0, 0.0)
        for s in range(n_loc)
    ]
    cut = min(256, cols)
    groups = [
        (lo, hi, [s for s in range(n_loc) if bounds[s] < hi and bounds[s + 1] > lo])
        for lo, hi in ((0, cut), (cut, cols))
        if lo < hi
    ]
    below = [jnp.where(col_ids < bounds[w + 1], 1.0, 0.0) for w in range(n_loc - 1)]
    q_prefix = jnp.concatenate([query * b.astype(BF) for b in below], axis=0)
    weight = jnp.transpose(weight_ref[...])

    for copy in fetches:
        copy.wait_recv()
    fetched = from_blocks(f_in)
    against = jnp.concatenate([fetched] + [doc] * (slots // ql), axis=0)
    rhs_t = (((1,), (1,)), ((), ()))
    top = lax.dot_general(query, against, rhs_t, preferred_element_type=F32)
    pos_row = jnp.sum(jnp.where(eye, top[:, slots:], 0.0), axis=0, keepdims=True)
    ex_out[0:ql, :] = top[:, :slots]
    ex_out[ql:, :] = jnp.broadcast_to(pos_row, (8, slots))
    s1 = alloc("s", n_mp - 1)
    t1 = alloc("r", n_mp - 1)
    shares = []
    for j in range(1, n_mp):
        copy = remote(ex_out, ex_in.at[m], s1 + j - 1, t1 + j - 1, mp=flip_bits(m, j))
        copy.start()
        shares.append(copy)
        sent.append(copy)
    spread(True, lambda copy: copy.start())

    def diagonal(level):
        return jnp.sum(jnp.where(eye, level, 0.0), axis=1, keepdims=True)

    def softmax(w, neg_score, pos_score):
        scale = scale_ref[w] * (1.0 / math.sqrt(bounds[w + 1]))
        neg_logit = jnp.where(named > 0.0, neg_score * scale, -1e30)
        pos_logit = pos_score * scale
        highest = jnp.maximum(jnp.max(neg_logit, axis=1, keepdims=True), pos_logit)
        neg_exp = named * jnp.exp(neg_logit - highest)
        pos_exp = jnp.exp(pos_logit - highest)
        denominator = jnp.sum(neg_exp, axis=1, keepdims=True) + pos_exp
        row_weight = weight[:, w : w + 1] * scale
        return (
            neg_exp * (row_weight / denominator),
            row_weight * (pos_exp / denominator - 1.0),
        )

    scores = lax.dot_general(q_prefix, against, rhs_t, preferred_element_type=F32)
    seg_neg = [None] * NW
    seg_pos = [None] * NW
    top_pos = diagonal(top[:, slots:])
    neg_run, pos_run = softmax(n_loc - 1, top[:, :slots], top_pos)
    seg_neg[n_loc - 1], seg_pos[n_loc - 1] = neg_run, pos_run
    for w in reversed(range(n_loc - 1)):
        level = scores[w * ql : (w + 1) * ql]
        neg_term, pos_term = softmax(w, level[:, :slots], diagonal(level[:, slots:]))
        neg_run, pos_run = neg_run + neg_term, pos_run + pos_term
        seg_neg[w], seg_pos[w] = neg_run, pos_run

    far = range(n_loc, NW)

    def inside_of(w, k):
        return jnp.where((k + 1) * cols <= bounds[w + 1], 1.0, 0.0)

    neg = {w: inside_of(w, m) * top[:, :slots] for w in far}
    pos = {w: inside_of(w, m) * top_pos for w in far}
    for j in range(1, n_mp):
        k = flip_bits(m, j)
        shares[j - 1].wait_recv()
        share = ex_in[k]
        other_neg = share[0:ql]
        other_pos = diagonal(jnp.broadcast_to(share[ql : ql + 1], (ql, slots)))
        for w in far:
            neg[w] = neg[w] + inside_of(w, k) * other_neg
            pos[w] = pos[w] + inside_of(w, k) * other_pos

    neg_run = jnp.zeros((ql, slots), F32)
    pos_run = jnp.zeros((ql, 1), F32)
    for w in reversed(far):
        neg_term, pos_term = softmax(w, neg[w], pos[w])
        neg_run, pos_run = neg_run + neg_term, pos_run + pos_term
        seg_neg[w], seg_pos[w] = neg_run, pos_run

    def local(values):
        low = [value + values[n_loc] for value in values[:n_loc]]
        mine = values[NW - 1]
        for s in reversed(range(n_loc, NW - 1)):
            mine = jnp.where((m + 1) * cols <= bounds[s + 1], values[s], mine)
        return [jnp.where(m == 0, low[0], mine)] + low[1:]

    columns = local(seg_pos)
    pos_cols = jnp.broadcast_to(columns[0], (ql, cols))
    for s in range(1, n_loc):
        here = jnp.logical_and(col_ids >= bounds[s], m == 0)
        pos_cols = jnp.where(here, columns[s], pos_cols)
    coef[...] = jnp.concatenate(local(seg_neg), axis=0).astype(BF)

    def part(s, n):
        return coef[s * ql : (s + n) * ql, :]

    @pl.when(m != 0)
    def _():
        term = lax.dot_general(part(0, 1), query, from_rows, preferred_element_type=F32)
        to_blocks(term, r_out)

    @pl.when(m == 0)
    def _():
        pieces = []
        for lo, hi, segs in groups:
            masked = [query[:, lo:hi] * seg[s][:, lo:hi].astype(BF) for s in segs]
            pieces.append(
                lax.dot_general(
                    part(segs[0], len(segs)),
                    jnp.concatenate(masked, axis=0),
                    from_rows,
                    preferred_element_type=F32,
                )
            )
        to_blocks(jnp.concatenate(pieces, axis=1), r_out)

    returns = exchange(lambda peer: r_out.at[peer], lambda peer: r_in.at[r])
    r_in[r] = r_out[r]

    @pl.when(m != 0)
    def _():
        term = jnp.dot(part(0, 1), fetched, preferred_element_type=F32)
        grads[r, 1] = (term + pos_cols * doc.astype(F32)).astype(BF)

    @pl.when(m == 0)
    def _():
        pieces = []
        for lo, hi, segs in groups:
            levels = jnp.dot(
                part(segs[0], len(segs)), fetched[:, lo:hi], preferred_element_type=F32
            )
            piece = levels[0:ql] * seg[segs[0]][:, lo:hi]
            for i in range(1, len(segs)):
                piece = piece + levels[i * ql : (i + 1) * ql] * seg[segs[i]][:, lo:hi]
            pieces.append(piece)
        term = jnp.concatenate(pieces, axis=1)
        grads[r, 1] = (term + pos_cols * doc.astype(F32)).astype(BF)

    rows = ql // parts

    def gather(h):
        return Gather(lambda o, c: grads.at[o, h, pl.ds(c * rows, rows)], parts)

    gather_q = gather(1)
    gather_q.start()

    def partial_start(h, between):
        s = alloc("s", n_mp - 1)
        t = alloc("r", n_mp - 1)
        copies = []
        value = grads[r, h]
        for j in [*range(2, n_mp), 1]:
            k = flip_bits(m, j)
            term = lax.dot_general(value, head_rows(k), rhs_t, preferred_element_type=F32)
            part_out[h, j - 1] = term.astype(BF)
            copy = remote(
                part_out.at[h, j - 1], part_in.at[h, j - 1], s + j - 1, t + j - 1, mp=k
            )
            copy.start()
            copies.append(copy)
            sent.append(copy)
            between(len(copies))
        mine = lax.dot_general(value, head_rows(m), rhs_t, preferred_element_type=F32)
        return copies, mine

    def partial_end(h, copies, mine):
        for j, copy in zip([*range(2, n_mp), 1], copies):
            copy.wait_recv()
            mine = mine + part_in[h, j - 1].astype(F32)
        return mine.astype(BF)

    part_q = partial_start(1, lambda n: None)
    hand_pass(0)
    hand_start(1)
    gather_q.forward(1)
    for copy in returns:
        copy.wait_recv()
    doc_back = jnp.dot(sel_t, from_blocks(r_in), preferred_element_type=F32)
    grads[r, 0] = (doc_back + pos_cols * query.astype(F32)).astype(BF)
    gather_d = gather(0)
    gather_d.start()
    gather_q.forward(*range(2, half - 1))
    part_d = partial_start(0, lambda n: None)
    gather_d.forward(1)
    gather_q.forward(*range(max(half - 1, 2), half))
    gather_d.forward(*range(2, half - 1))
    hand_pass(1)
    qg_ref[...] = partial_end(1, *part_q)
    hand_end(0)
    hand_end(1)
    gather_q.drain()
    gather_d.forward(*range(max(half - 1, 2), half))
    dg_ref[...] = partial_end(0, *part_d)
    for k in range(half):
        line = lax.rem(place + k, half)
        gather_q.finish(line)
        gather_d.finish(line)
        both = jnp.concatenate([rows_t[0, line], rows_t[1, line]], axis=1)
        term = jnp.dot(
            both,
            grads[pl.ds(line * 2, 2)].reshape(4 * ql, cols),
            preferred_element_type=F32,
        )
        if k == 0:
            hg_ref[...] = term
        else:
            hg_ref[...] += term

    for copy in sent:
        copy.wait_send()
    gather_d.drain()
    spread(False, lambda copy: copy.wait_send())
    spread(True, lambda copy: copy.wait_send())

    @pl.when(m == keeper)
    def _():
        for copy in halves[0] + halves[1]:
            copy.wait_send()

    @pl.when(passes)
    def _():
        halves[0][-1].wait_send()
        halves[1][-1].wait_send()


def hand_on(*refs):
    for src, dst in zip(refs[: len(refs) // 2], refs[len(refs) // 2 :]):
        dst[...] = src[...]


def solution(mesh):
    n_dp = mesh.shape["dp"]
    n_mp = mesh.shape["mp"]

    def on_device(query_rows, doc_rows, head, logit_scale, loss_grad, shortlist, send_rows):
        ql, cols = query_rows.shape
        total = n_mp * cols
        slots = send_rows.shape[1]
        blk = slots // n_dp
        chunk = total // n_dp
        n_loc = local_segments(width_bounds(total), cols)
        n_send = 7 * (n_mp - 1) + n_dp // n_mp + 2 * (n_dp - 1) + 2 * PARTS * (2 * n_dp - 1)
        n_recv = 5 * (n_mp - 1) + n_dp + 2 * (n_dp - 1) + 2 + 2 * PARTS * n_dp
        vmem = pl.BlockSpec(memory_space=pltpu.VMEM)
        shapes = (
            jax.ShapeDtypeStruct((ql, cols), BF),
            jax.ShapeDtypeStruct((ql, cols), BF),
            jax.ShapeDtypeStruct((chunk, cols), F32),
        )
        found = pl.pallas_call(
            functools.partial(kernel, n_dp, n_mp),
            out_shape=shapes,
            in_specs=[pl.BlockSpec(memory_space=pltpu.HBM)] * 7,
            out_specs=(vmem, vmem, vmem),
            scratch_shapes=[
                pltpu.VMEM((ql, cols), BF),
                pltpu.VMEM((ql, cols), BF),
                pltpu.SMEM(logit_scale.shape, F32),
                pltpu.VMEM(loss_grad.shape[::-1], F32),
                pltpu.VMEM(shortlist.shape, jnp.int32),
                pltpu.VMEM(send_rows.shape, jnp.int32),
                pltpu.VMEM((total, cols), BF),
                pltpu.VMEM((n_mp, 2, ql, cols), BF),
                pltpu.VMEM((cols, 2 * ql), BF),
                pltpu.VMEM((2, n_dp // 2, chunk, 2 * ql), BF),
                pltpu.VMEM((n_dp, blk, cols), BF),
                pltpu.VMEM((n_dp, blk, cols), BF),
                pltpu.VMEM((ql + 8, slots), F32),
                pltpu.VMEM((n_mp, ql + 8, slots), F32),
                pltpu.VMEM((n_loc * ql, slots), BF),
                pltpu.VMEM((n_dp, blk, cols), BF),
                pltpu.VMEM((n_dp, blk, cols), BF),
                pltpu.VMEM((n_dp, 2, ql, cols), BF),
                pltpu.VMEM((2, n_mp - 1, ql, cols), BF),
                pltpu.VMEM((2, n_mp - 1, ql, cols), BF),
                pltpu.VMEM((slots, cols), F32),
                pltpu.SemaphoreType.DMA((n_send,)),
                pltpu.SemaphoreType.DMA((n_recv,)),
                pltpu.SemaphoreType.DMA((8,)),
            ],
            compiler_params=pltpu.CompilerParams(
                collective_id=0, has_side_effects=True, vmem_limit_bytes=48 << 20
            ),
        )(
            *[
                pltpu.with_memory_space_constraint(x, pltpu.HBM)
                for x in (
                    query_rows,
                    doc_rows,
                    head,
                    logit_scale,
                    loss_grad.T,
                    shortlist,
                    send_rows,
                )
            ]
        )
        return pl.pallas_call(
            hand_on,
            out_shape=shapes,
            in_specs=[vmem] * 3,
            out_specs=(vmem,) * 3,
            compiler_params=pltpu.CompilerParams(vmem_limit_bytes=8 << 20),
        )(*found)

    return jax.shard_map(
        on_device,
        mesh=mesh,
        in_specs=(
            P("dp", "mp"),
            P("dp", "mp"),
            P(None, "mp"),
            P(),
            P("dp", None),
            P("dp", None),
            P("dp", None),
        ),
        out_specs=(P("dp", "mp"), P("dp", "mp"), P("dp", "mp")),
        check_vma=False,
    )
```

time: 48.7 us -> 46.3 us (0.951)
  Pallas kernels: 48 us -> 45.5 us
    pallas_call x1, Pallas kernels: 46.9 us -> 44.5 us  [on_device(): pl.pallas_call(functools.partial(kernel, n_dp, n_mp), out_shape=shapes, i...]
where the time goes in v1:
time: 46.3 us; the launch traced here: 46.2 us
  Pallas kernels  45.5 us (98%)
  between operations  0.64 us (1%)
    pallas_call x1, Pallas kernels, on_device(): pl.pallas_call(functools.partial(kernel, n_dp, n_mp), out_shape=shapes, i...  44.5 us
    pallas_call x1, Pallas kernels, on_device(): pl.pallas_call(hand_on, out_shape=shapes, in_specs=[vmem] * 3, out_specs=...  1.01 us

profile of v1, /device:TPU:0, one launch (start us, length us, event | category | flops | bytes accessed | tf_op | source)
XLA Modules:
  0.0 46.2 jit_solution(13328268498453556313)
XLA Ops:
  0.6 44.5 %shard_map.94 = (bf16[64,640]{1,0:T(8,128)(2,1)S(1)}, bf16[64,640]{1,0:T(8,128)(2,1)S(1)}, f32[320,640]{1,0:T(8,128)S(1)}) custom-call(bf16[64,640]{1,0:T(8,128)(2,1)} %q_hbm.1, bf16[64,640]{1,0:T(8,128)(2,1)} %d_hbm.1, bf16[2560,640]{1,0:T(8,128)(2,1)} %head_hbm.1, f32[7]{0:T(128)} %scale_hbm.1, f32[7,64]{1,0:T(8,128)} %bitcast.1, s32[64,128]{1,0:T(8,128)} %short_hbm.1, ...), custom_call_target="tpu_custom_call" | custom-call | tf_op jit(solution)/shard_map/pallas_call | solution.py:646
  45.1 1.0 %shard_map.95 = (bf16[64,640]{1,0:T(8,128)(2,1)}, bf16[64,640]{1,0:T(8,128)(2,1)}, f32[320,640]{1,0:T(8,128)}) custom-call(bf16[64,640]{1,0:T(8,128)(2,1)S(1)} %get-tuple-element.6.refs_0_, bf16[64,640]{1,0:T(8,128)(2,1)S(1)} %get-tuple-element.7.refs_1_, f32[320,640]{1,0:T(8,128)S(1)} %get-tuple-element.8.refs_2_), custom_call_target="tpu_custom_call" | custom-call | tf_op jit(solution)/shard_map/pallas_call | solution.py:694

commit v2 on v1

--- a/solution.py
+++ b/solution.py
@@ -130,10 +130,25 @@
         copy.wait()
     pl.semaphore_wait(barrier, n_mp - 1 + n_dp - 1)
 
-    sent = []
     parts = PARTS
 
-    s0 = alloc("s", 2 * (n_mp - 1))
+    def sent_rows(s, n):
+        ref = head.at[pl.ds(0, n)]
+        remote(ref, ref, s, 0, dp=partner).wait_send()
+
+    def came_rows(t, n):
+        ref = head.at[pl.ds(0, n)]
+        remote(ref, ref, 0, t, dp=partner).wait_recv()
+
+    def sent_blocks(pair):
+        ref = f_in.at[pl.ds(0, n_dp - 1)]
+        remote(ref, ref, *pair, dp=partner).wait_send()
+
+    def came_blocks(pair):
+        ref = f_in.at[pl.ds(0, n_dp - 1)]
+        remote(ref, ref, *pair, dp=partner).wait_recv()
+
+    s0 = alloc("s", 1)
     t0 = alloc("r", 2 * (n_mp - 1))
     row_copies = []
     for h, ref in enumerate((d_ref, q_ref)):
@@ -141,7 +156,7 @@
         copies = {}
         for j in [*range(2, n_mp, 2), 1]:
             copies[j] = remote(
-                ref, whole.at[m, h], s0 + base + j, t0 + base + j, mp=flip_bits(m, j)
+                ref, whole.at[m, h], s0, t0 + base + j, mp=flip_bits(m, j)
             )
             copies[j].start()
         for j in range(2, n_mp, 2):
@@ -149,29 +164,24 @@
             copies[j + 1] = remote(
                 whole.at[k, h],
                 whole.at[k, h],
-                s0 + base + j + 1,
+                s0,
                 t0 + base + j + 1,
                 mp=flip_bits(m, 1),
             )
         row_copies.append(copies)
-        sent.extend(copies.values())
 
     def exchange(out, into):
-        s = alloc("s", n_dp - 1)
-        t = alloc("r", n_dp - 1)
-        copies = []
+        s = alloc("s", 1)
+        t = alloc("r", 1)
         for k in range(1, n_dp):
             peer = lax.rem(r + k, n_dp)
-            copy = remote(out(peer), into(peer), s + k - 1, t + k - 1, dp=peer)
-            copy.start()
-            copies.append(copy)
-            sent.append(copy)
-        return copies
+            remote(out(peer), into(peer), s, t, dp=peer).start()
+        return s, t
 
     own = jnp.concatenate([d_ref[...], q_ref[...]], axis=0)
     own_t[...] = jnp.transpose(own)
     s_t = alloc("s", per_mp)
-    t_t = alloc("r", n_dp)
+    t_t = alloc("r", 2)
     place = lax.div(r, 2)
     side = lax.rem(r, 2)
     keeper = lax.div(r, per_mp)
@@ -184,7 +194,7 @@
                 own_t.at[pl.ds(pl.multiple_of(c * chunk, 16), chunk)],
                 rows_t.at[side, place],
                 s_t + 2 * i + int(late),
-                t_t + r,
+                t_t + int(late),
                 dp=target,
             )
             if late:
@@ -199,16 +209,15 @@
         c = lax.rem(r, per_mp)
         rows_t[side, place] = own_t[pl.ds(pl.multiple_of(c * chunk, 16), chunk), :]
 
-    s_f = alloc("s", 2 * (n_mp - 1))
+    s_f = alloc("s", 2)
     t_f = alloc("r", 2)
     same = lax.rem(m, 2) == lax.rem(keeper, 2)
     passes = jnp.logical_and(same, m != keeper)
 
     def hand_over(late):
         ref = rows_t.at[1 - side if late else side]
-        first = s_f + int(late) * (n_mp - 1) - 1
         return [
-            remote(ref, ref, first + j, t_f + int(late), mp=flip_bits(m, j))
+            remote(ref, ref, s_f + int(late), t_f + int(late), mp=flip_bits(m, j))
             for j in [*range(2, n_mp, 2), 1]
         ]
 
@@ -217,19 +226,8 @@
     def hand_start(late):
         @pl.when(m == keeper)
         def _():
-            for p in range(half):
-                origin = 2 * p + (1 - side if late else side)
-
-                @pl.when(r != origin)
-                def _(p=p, origin=origin):
-                    remote(
-                        own_t.at[pl.ds(0, chunk)],
-                        rows_t.at[1 - side if late else side, p],
-                        s_t,
-                        t_t + origin,
-                        dp=r,
-                    ).wait_recv()
-
+            n = half if late else half - 1
+            came_rows(t_t + int(late), n * chunk * 2 * ql // cols)
             for copy in halves[late]:
                 copy.start()
 
@@ -261,13 +259,13 @@
                 acc = acc + jnp.dot(whole[k, h], head_rows(k), preferred_element_type=F32)
         return acc.astype(BF)
 
+    s_g = alloc("s", 2)
+    t_g = alloc("r", half)
+
     class Gather:
-        def __init__(self, piece, parts):
-            self.piece = piece
-            self.parts = parts
-            self.s = alloc("s", parts * (4 * half - 1))
-            self.t = alloc("r", parts * 2 * half)
-            self.used = 0
+        def __init__(self, h):
+            self.h = h
+            self.t = alloc("r", parts * half)
             self.own = [
                 ([self.copy(r, c, dz) for c in range(parts)], self.within(dz))
                 for dz in (-1, 1)
@@ -282,19 +280,18 @@
                         (self.copy(origin, c, dz), self.copy(origin, c, 0))
                         for c in range(parts)
                     ]
-                    self.hops[d].append((origin, self.within(-dz * d), self.within(dz), steps))
+                    self.hops[d].append((self.within(-dz * d), self.within(dz), steps))
 
         def within(self, step):
             return place + step >= 0 if step < 0 else place + step < half
 
         def copy(self, origin, c, dz):
-            ref = self.piece(origin, c)
-            row = lax.div(origin, 2) + (half if dz == 0 else 0)
+            rows = ql // parts
+            ref = grads.at[origin, self.h, pl.ds(c * rows, rows)]
+            line = lax.div(origin, 2)
             target = lax.rem(r + 2 * dz + n_dp, n_dp) if dz else partner
-            self.used += 1
-            return remote(
-                ref, ref, self.s + self.used - 1, self.t + row * self.parts + c, dp=target
-            )
+            t = self.t + line * parts + c if dz else t_g + line
+            return remote(ref, ref, s_g + self.h, t, dp=target)
 
         def start(self):
             for copies, inside in self.own:
@@ -309,7 +306,7 @@
 
         def forward(self, *hops):
             for d in hops:
-                for origin, there, further, steps in self.hops[d]:
+                for there, further, steps in self.hops[d]:
 
                     @pl.when(there)
                     def _(further=further, steps=steps):
@@ -317,38 +314,6 @@
                             relay.wait_recv()
                             pl.when(further)(relay.start)
                             over.start()
-
-        def finish(self, line):
-            for c in range(self.parts):
-                self.copy_from_partner(line, c).wait_recv()
-
-        def copy_from_partner(self, line, c):
-            ref = self.piece(line * 2 + 1 - side, c)
-            row = self.t + (line + half) * self.parts + c
-            return remote(ref, ref, self.s, row, dp=partner)
-
-        def drain(self):
-            for copies, inside in self.own:
-
-                @pl.when(inside)
-                def _(copies=copies):
-                    for copy in copies:
-                        copy.wait_send()
-
-            for copy in self.across:
-                copy.wait_send()
-            for hops in self.hops.values():
-                for origin, there, further, steps in hops:
-
-                    @pl.when(there)
-                    def _(further=further, steps=steps):
-                        for _, over in steps:
-                            over.wait_send()
-
-                        @pl.when(further)
-                        def _():
-                            for relay, _ in steps:
-                                relay.wait_send()
 
     slot_ids = lax.broadcasted_iota(jnp.int32, (ql, slots), 1)
     row_ids = lax.broadcasted_iota(jnp.int32, (ql, slots), 0)
@@ -401,8 +366,7 @@
     q_prefix = jnp.concatenate([query * b.astype(BF) for b in below], axis=0)
     weight = jnp.transpose(weight_ref[...])
 
-    for copy in fetches:
-        copy.wait_recv()
+    came_blocks(fetches)
     fetched = from_blocks(f_in)
     against = jnp.concatenate([fetched] + [doc] * (slots // ql), axis=0)
     rhs_t = (((1,), (1,)), ((), ()))
@@ -410,14 +374,13 @@
     pos_row = jnp.sum(jnp.where(eye, top[:, slots:], 0.0), axis=0, keepdims=True)
     ex_out[0:ql, :] = top[:, :slots]
     ex_out[ql:, :] = jnp.broadcast_to(pos_row, (8, slots))
-    s1 = alloc("s", n_mp - 1)
+    s1 = alloc("s", 1)
     t1 = alloc("r", n_mp - 1)
     shares = []
     for j in range(1, n_mp):
-        copy = remote(ex_out, ex_in.at[m], s1 + j - 1, t1 + j - 1, mp=flip_bits(m, j))
+        copy = remote(ex_out, ex_in.at[m], s1, t1 + j - 1, mp=flip_bits(m, j))
         copy.start()
         shares.append(copy)
-        sent.append(copy)
     spread(True, lambda copy: copy.start())
 
     def diagonal(level):
@@ -532,65 +495,50 @@
         term = jnp.concatenate(pieces, axis=1)
         grads[r, 1] = (term + pos_cols * doc.astype(F32)).astype(BF)
 
-    rows = ql // parts
-
-    def gather(h):
-        return Gather(lambda o, c: grads.at[o, h, pl.ds(c * rows, rows)], parts)
-
-    gather_q = gather(1)
+    gather_q = Gather(1)
     gather_q.start()
 
-    def partial_start(h, between):
-        s = alloc("s", n_mp - 1)
-        t = alloc("r", n_mp - 1)
-        copies = []
+    s_p = alloc("s", 1)
+    t_p = alloc("r", 2)
+
+    def partial_start(h):
         value = grads[r, h]
         for j in [*range(2, n_mp), 1]:
             k = flip_bits(m, j)
             term = lax.dot_general(value, head_rows(k), rhs_t, preferred_element_type=F32)
             part_out[h, j - 1] = term.astype(BF)
-            copy = remote(
-                part_out.at[h, j - 1], part_in.at[h, j - 1], s + j - 1, t + j - 1, mp=k
-            )
-            copy.start()
-            copies.append(copy)
-            sent.append(copy)
-            between(len(copies))
-        mine = lax.dot_general(value, head_rows(m), rhs_t, preferred_element_type=F32)
-        return copies, mine
-
-    def partial_end(h, copies, mine):
-        for j, copy in zip([*range(2, n_mp), 1], copies):
-            copy.wait_recv()
+            remote(part_out.at[h, j - 1], part_in.at[h, j - 1], s_p, t_p + h, mp=k).start()
+        return lax.dot_general(value, head_rows(m), rhs_t, preferred_element_type=F32)
+
+    def partial_end(h, mine):
+        came_rows(t_p + h, (n_mp - 1) * ql)
+        for j in range(1, n_mp):
             mine = mine + part_in[h, j - 1].astype(F32)
         return mine.astype(BF)
 
-    part_q = partial_start(1, lambda n: None)
+    part_q = partial_start(1)
     hand_pass(0)
     hand_start(1)
-    gather_q.forward(1)
-    for copy in returns:
-        copy.wait_recv()
+    came_blocks(returns)
     doc_back = jnp.dot(sel_t, from_blocks(r_in), preferred_element_type=F32)
     grads[r, 0] = (doc_back + pos_cols * query.astype(F32)).astype(BF)
-    gather_d = gather(0)
+    gather_d = Gather(0)
     gather_d.start()
+    gather_q.forward(1)
+    part_d = partial_start(0)
     gather_q.forward(*range(2, half - 1))
-    part_d = partial_start(0, lambda n: None)
     gather_d.forward(1)
     gather_q.forward(*range(max(half - 1, 2), half))
     gather_d.forward(*range(2, half - 1))
     hand_pass(1)
-    qg_ref[...] = partial_end(1, *part_q)
+    qg_ref[...] = partial_end(1, part_q)
     hand_end(0)
     hand_end(1)
-    gather_q.drain()
     gather_d.forward(*range(max(half - 1, 2), half))
-    dg_ref[...] = partial_end(0, *part_d)
+    dg_ref[...] = partial_end(0, part_d)
     for k in range(half):
         line = lax.rem(place + k, half)
-        gather_q.finish(line)
-        gather_d.finish(line)
+        came_rows(t_g + line, 2 * ql)
         both = jnp.concatenate([rows_t[0, line], rows_t[1, line]], axis=1)
         term = jnp.dot(
             both,
@@ -602,21 +550,37 @@
         else:
             hg_ref[...] += term
 
-    for copy in sent:
-        copy.wait_send()
-    gather_d.drain()
+    inner = jnp.logical_and(place > 0, place < half - 1)
+
+    @pl.when(inner)
+    def _():
+        for h in (0, 1):
+            sent_rows(s_g + h, ql * (2 * half + 1))
+
+    @pl.when(jnp.logical_not(inner))
+    def _():
+        for h in (0, 1):
+            sent_rows(s_g + h, ql * (half + 1))
+
+    sent_rows(s0, 2 * (n_mp - 1) * ql)
+    sent_blocks(fetches)
+    sent_blocks(returns)
+    sent_rows(s_p, 2 * (n_mp - 1) * ql)
+    others = ex_in.at[pl.ds(0, n_mp - 1)]
+    remote(others, others, s1, 0, dp=partner).wait_send()
     spread(False, lambda copy: copy.wait_send())
     spread(True, lambda copy: copy.wait_send())
+    half_rows = half * chunk * 2 * ql // cols
 
     @pl.when(m == keeper)
     def _():
-        for copy in halves[0] + halves[1]:
-            copy.wait_send()
+        for late in (0, 1):
+            sent_rows(s_f + late, n_mp // 2 * half_rows)
 
     @pl.when(passes)
     def _():
-        halves[0][-1].wait_send()
-        halves[1][-1].wait_send()
+        for late in (0, 1):
+            sent_rows(s_f + late, half_rows)
 
 
 def hand_on(*refs):
@@ -635,8 +599,8 @@
         blk = slots // n_dp
         chunk = total // n_dp
         n_loc = local_segments(width_bounds(total), cols)
-        n_send = 7 * (n_mp - 1) + n_dp // n_mp + 2 * (n_dp - 1) + 2 * PARTS * (2 * n_dp - 1)
-        n_recv = 5 * (n_mp - 1) + n_dp + 2 * (n_dp - 1) + 2 + 2 * PARTS * n_dp
+        n_send = 9 + n_dp // n_mp
+        n_recv = 3 * (n_mp - 1) + 8 + n_dp // 2 + PARTS * n_dp
         vmem = pl.BlockSpec(memory_space=pltpu.VMEM)
         shapes = (
             jax.ShapeDtypeStruct((ql, cols), BF),

time: 46.3 us -> 43.9 us (0.948)
  Pallas kernels: 45.5 us -> 43.1 us
    pallas_call x1, Pallas kernels: 44.5 us -> 42.1 us  [on_device(): pl.pallas_call(functools.partial(kernel, n_dp, n_mp), out_shape=shapes, i...]
where the time goes in v2:
time: 43.9 us; the launch traced here: 43.7 us
  Pallas kernels  43.1 us (98%)
  between operations  0.64 us (1%)
    pallas_call x1, Pallas kernels, on_device(): pl.pallas_call(functools.partial(kernel, n_dp, n_mp), out_shape=shapes, i...  42.1 us
    pallas_call x1, Pallas kernels, on_device(): pl.pallas_call(hand_on, out_shape=shapes, in_specs=[vmem] * 3, out_specs=...  1.01 us

profile of v2, /device:TPU:0, one launch (start us, length us, event | category | flops | bytes accessed | tf_op | source)
XLA Modules:
  0.0 43.7 jit_solution(9015631435770812162)
XLA Ops:
  0.6 42.1 %shard_map.94 = (bf16[64,640]{1,0:T(8,128)(2,1)S(1)}, bf16[64,640]{1,0:T(8,128)(2,1)S(1)}, f32[320,640]{1,0:T(8,128)S(1)}) custom-call(bf16[64,640]{1,0:T(8,128)(2,1)} %q_hbm.1, bf16[64,640]{1,0:T(8,128)(2,1)} %d_hbm.1, bf16[2560,640]{1,0:T(8,128)(2,1)} %head_hbm.1, f32[7]{0:T(128)} %scale_hbm.1, f32[7,64]{1,0:T(8,128)} %bitcast.1, s32[64,128]{1,0:T(8,128)} %short_hbm.1, ...), custom_call_target="tpu_custom_call" | custom-call | tf_op jit(solution)/shard_map/pallas_call | solution.py:610
  42.7 1.0 %shard_map.95 = (bf16[64,640]{1,0:T(8,128)(2,1)}, bf16[64,640]{1,0:T(8,128)(2,1)}, f32[320,640]{1,0:T(8,128)}) custom-call(bf16[64,640]{1,0:T(8,128)(2,1)S(1)} %get-tuple-element.6.refs_0_, bf16[64,640]{1,0:T(8,128)(2,1)S(1)} %get-tuple-element.7.refs_1_, f32[320,640]{1,0:T(8,128)S(1)} %get-tuple-element.8.refs_2_), custom_call_target="tpu_custom_call" | custom-call | tf_op jit(solution)/shard_map/pallas_call | solution.py:658

commit v3 on v2

--- a/solution.py
+++ b/solution.py
@@ -154,18 +154,18 @@
     for h, ref in enumerate((d_ref, q_ref)):
         base = h * (n_mp - 1) - 1
         copies = {}
-        for j in [*range(2, n_mp, 2), 1]:
+        for j in [*range(3, n_mp, 2), 1]:
             copies[j] = remote(
                 ref, whole.at[m, h], s0, t0 + base + j, mp=flip_bits(m, j)
             )
             copies[j].start()
-        for j in range(2, n_mp, 2):
+        for j in range(3, n_mp, 2):
             k = flip_bits(m, j)
-            copies[j + 1] = remote(
+            copies[j - 1] = remote(
                 whole.at[k, h],
                 whole.at[k, h],
                 s0,
-                t0 + base + j + 1,
+                t0 + base + j - 1,
                 mp=flip_bits(m, 1),
             )
         row_copies.append(copies)
@@ -251,11 +251,11 @@
         copies = row_copies[h]
         acc = jnp.dot(ref[...], head_rows(m), preferred_element_type=F32)
         for j in range(1, n_mp, 2):
-            for i in [j] if j == 1 else [j - 1, j]:
+            for i in [j] if j == 1 else [j, j - 1]:
                 k = flip_bits(m, i)
                 copies[i].wait_recv()
-                if i % 2 == 0:
-                    copies[i + 1].start()
+                if i != 1 and i % 2 == 1:
+                    copies[i - 1].start()
                 acc = acc + jnp.dot(whole[k, h], head_rows(k), preferred_element_type=F32)
         return acc.astype(BF)
 

time: 43.9 us -> 43.1 us (0.982)
  Pallas kernels: 43.1 us -> 42.3 us
    pallas_call x1, Pallas kernels: 42.1 us -> 41.3 us  [on_device(): pl.pallas_call(functools.partial(kernel, n_dp, n_mp), out_shape=shapes, i...]
where the time goes in v3:
time: 43.1 us; the launch traced here: 42.9 us
  Pallas kernels  42.3 us (98%)
  between operations  0.64 us (1%)
    pallas_call x1, Pallas kernels, on_device(): pl.pallas_call(functools.partial(kernel, n_dp, n_mp), out_shape=shapes, i...  41.3 us
    pallas_call x1, Pallas kernels, on_device(): pl.pallas_call(hand_on, out_shape=shapes, in_specs=[vmem] * 3, out_specs=...  1.01 us

profile of v3, /device:TPU:0, one launch (start us, length us, event | category | flops | bytes accessed | tf_op | source)
XLA Modules:
  0.0 42.9 jit_solution(1926662625639091919)
XLA Ops:
  0.6 41.3 %shard_map.94 = (bf16[64,640]{1,0:T(8,128)(2,1)S(1)}, bf16[64,640]{1,0:T(8,128)(2,1)S(1)}, f32[320,640]{1,0:T(8,128)S(1)}) custom-call(bf16[64,640]{1,0:T(8,128)(2,1)} %q_hbm.1, bf16[64,640]{1,0:T(8,128)(2,1)} %d_hbm.1, bf16[2560,640]{1,0:T(8,128)(2,1)} %head_hbm.1, f32[7]{0:T(128)} %scale_hbm.1, f32[7,64]{1,0:T(8,128)} %bitcast.1, s32[64,128]{1,0:T(8,128)} %short_hbm.1, ...), custom_call_target="tpu_custom_call" | custom-call | tf_op jit(solution)/shard_map/pallas_call | solution.py:610
  41.9 1.0 %shard_map.95 = (bf16[64,640]{1,0:T(8,128)(2,1)}, bf16[64,640]{1,0:T(8,128)(2,1)}, f32[320,640]{1,0:T(8,128)}) custom-call(bf16[64,640]{1,0:T(8,128)(2,1)S(1)} %get-tuple-element.6.refs_0_, bf16[64,640]{1,0:T(8,128)(2,1)S(1)} %get-tuple-element.7.refs_1_, f32[320,640]{1,0:T(8,128)S(1)} %get-tuple-element.8.refs_2_), custom_call_target="tpu_custom_call" | custom-call | tf_op jit(solution)/shard_map/pallas_call | solution.py:658

commit v4 on v3

--- a/solution.py
+++ b/solution.py
@@ -526,10 +526,10 @@
     gather_d.start()
     gather_q.forward(1)
     part_d = partial_start(0)
+    gather_d.forward(1)
     gather_q.forward(*range(2, half - 1))
-    gather_d.forward(1)
+    gather_d.forward(*range(2, half - 1))
     gather_q.forward(*range(max(half - 1, 2), half))
-    gather_d.forward(*range(2, half - 1))
     hand_pass(1)
     qg_ref[...] = partial_end(1, part_q)
     hand_end(0)

time: 43.1 us -> 41.8 us (0.970)
  Pallas kernels: 42.3 us -> 41.1 us
    pallas_call x1, Pallas kernels: 41.3 us -> 40 us  [on_device(): pl.pallas_call(functools.partial(kernel, n_dp, n_mp), out_shape=shapes, i...]
where the time goes in v4:
time: 41.8 us; the launch traced here: 41.7 us
  Pallas kernels  41.1 us (98%)
  between operations  0.64 us (2%)
    pallas_call x1, Pallas kernels, on_device(): pl.pallas_call(functools.partial(kernel, n_dp, n_mp), out_shape=shapes, i...  40 us
    pallas_call x1, Pallas kernels, on_device(): pl.pallas_call(hand_on, out_shape=shapes, in_specs=[vmem] * 3, out_specs=...  1.01 us

profile of v4, /device:TPU:0, one launch (start us, length us, event | category | flops | bytes accessed | tf_op | source)
XLA Modules:
  0.0 41.7 jit_solution(12830113455626677895)
XLA Ops:
  0.6 40.0 %shard_map.94 = (bf16[64,640]{1,0:T(8,128)(2,1)S(1)}, bf16[64,640]{1,0:T(8,128)(2,1)S(1)}, f32[320,640]{1,0:T(8,128)S(1)}) custom-call(bf16[64,640]{1,0:T(8,128)(2,1)} %q_hbm.1, bf16[64,640]{1,0:T(8,128)(2,1)} %d_hbm.1, bf16[2560,640]{1,0:T(8,128)(2,1)} %head_hbm.1, f32[7]{0:T(128)} %scale_hbm.1, f32[7,64]{1,0:T(8,128)} %bitcast.1, s32[64,128]{1,0:T(8,128)} %short_hbm.1, ...), custom_call_target="tpu_custom_call" | custom-call | tf_op jit(solution)/shard_map/pallas_call | solution.py:610
  40.7 1.0 %shard_map.95 = (bf16[64,640]{1,0:T(8,128)(2,1)}, bf16[64,640]{1,0:T(8,128)(2,1)}, f32[320,640]{1,0:T(8,128)}) custom-call(bf16[64,640]{1,0:T(8,128)(2,1)S(1)} %get-tuple-element.6.refs_0_, bf16[64,640]{1,0:T(8,128)(2,1)S(1)} %get-tuple-element.7.refs_1_, f32[320,640]{1,0:T(8,128)S(1)} %get-tuple-element.8.refs_2_), custom_call_target="tpu_custom_call" | custom-call | tf_op jit(solution)/shard_map/pallas_call | solution.py:658

commit v5 on v4

--- a/solution.py
+++ b/solution.py
@@ -584,8 +584,12 @@
 
 
 def hand_on(*refs):
-    for src, dst in zip(refs[: len(refs) // 2], refs[len(refs) // 2 :]):
-        dst[...] = src[...]
+    n = len(refs) // 2
+    copies = [pltpu.make_async_copy(refs[i], refs[n + i], refs[-1].at[i]) for i in range(n)]
+    for copy in reversed(copies):
+        copy.start()
+    for copy in copies:
+        copy.wait()
 
 
 def solution(mesh):
@@ -659,7 +663,8 @@
             hand_on,
             out_shape=shapes,
             in_specs=[vmem] * 3,
-            out_specs=(vmem,) * 3,
+            out_specs=(pl.BlockSpec(memory_space=pltpu.HBM),) * 3,
+            scratch_shapes=[pltpu.SemaphoreType.DMA((3,))],
             compiler_params=pltpu.CompilerParams(vmem_limit_bytes=8 << 20),
         )(*found)
 

time: 41.8 us -> 41.8 us (level)
  no operation moved by 1% of the time
where the time goes in v5:
time: 41.8 us; the launch traced here: 41.7 us
  Pallas kernels  41 us (98%)
  between operations  0.64 us (2%)
    pallas_call x1, Pallas kernels, on_device(): pl.pallas_call(functools.partial(kernel, n_dp, n_mp), out_shape=shapes, i...  40 us
    pallas_call x1, Pallas kernels, on_device(): pl.pallas_call(hand_on, out_shape=shapes, in_specs=[vmem] * 3, out_specs=...  0.96 us

profile of v5, /device:TPU:0, one launch (start us, length us, event | category | flops | bytes accessed | tf_op | source)
XLA Modules:
  0.0 41.7 jit_solution(784486345417445000)
XLA Ops:
  0.6 40.0 %shard_map.94 = (bf16[64,640]{1,0:T(8,128)(2,1)S(1)}, bf16[64,640]{1,0:T(8,128)(2,1)S(1)}, f32[320,640]{1,0:T(8,128)S(1)}) custom-call(bf16[64,640]{1,0:T(8,128)(2,1)} %q_hbm.1, bf16[64,640]{1,0:T(8,128)(2,1)} %d_hbm.1, bf16[2560,640]{1,0:T(8,128)(2,1)} %head_hbm.1, f32[7]{0:T(128)} %scale_hbm.1, f32[7,64]{1,0:T(8,128)} %bitcast.1, s32[64,128]{1,0:T(8,128)} %short_hbm.1, ...), custom_call_target="tpu_custom_call" | custom-call | tf_op jit(solution)/shard_map/pallas_call | solution.py:614
  40.7 1.0 %shard_map.95 = (bf16[64,640]{1,0:T(8,128)(2,1)}, bf16[64,640]{1,0:T(8,128)(2,1)}, f32[320,640]{1,0:T(8,128)}) custom-call(bf16[64,640]{1,0:T(8,128)(2,1)S(1)} %get-tuple-element.6.refs_0_, bf16[64,640]{1,0:T(8,128)(2,1)S(1)} %get-tuple-element.7.refs_1_, f32[320,640]{1,0:T(8,128)S(1)} %get-tuple-element.8.refs_2_), custom_call_target="tpu_custom_call" | custom-call | tf_op jit(solution)/shard_map/pallas_call | solution.py:662
